TPU v7x, 32 devices: a whole 2x2x4 slice. The times are simulated.
32 devices in a mesh: blk: 2 (over x), wide: 16 (over z, y, core).
Axes of the slice: x: 2, y: 2, z: 4, core: 2. Of those that a mesh axis runs over, the one named last changes fastest.
Arguments:
- volume: float32 [2, 2, 512, 896], P('blk', None, 'wide'), may hold values from -1.6 to 1.6
- path_lengths: float32 [2, 2, 2], replicated, may hold values from 0.5 to 2
- probe: float32 [2, 128, 128], replicated, may hold values from -6 to 6
- measured: bfloat16 [2, 16, 14, 128, 128], P('blk', 'wide'), may hold values from 0.19921875 to 3
- jitter: int32 [2, 2, 16, 14], P(None, 'blk', 'wide'), may hold values from 0 to 15
- step_sizes: float32 [2], replicated, may hold values from 0.02 to 0.2
Outputs:
- new_volume: float32 [2, 2, 512, 896], P('blk', None, 'wide')
- misfit: float32 [], replicated
All inputs are finite; a program needn't handle non-finite values.
Results may differ from a plain program's by a relative error of at most 0.0003.
Values sent between devices are 32-bit elements; how exact they have to be, the bound alone decides.
A program may use at most 64 MiB of HBM per device.

v0:
```python
import math
import jax
import jax.numpy as jnp
from jax import lax
from jax.sharding import PartitionSpec as P

ROWS_DEV = 32
PATCH = 128
CSTEP = 64
highest = lax.Precision.HIGHEST
floor_value = 0.25


def passed_along(value, axis, steps):
    count = lax.axis_size(axis)
    pairs = [(source, (source + steps) % count) for source in range(count)]
    return lax.ppermute(value, axis, pairs)


def from_behind(shard, axis, by):
    count = lax.axis_size(axis)
    pairs = [(i, i + by) for i in range(count) if 0 <= i + by < count]
    return lax.ppermute(shard, axis, pairs)


def dft_tables(length):
    grid = jnp.arange(length, dtype=jnp.int32)
    product = grid[:, None] * grid[None, :] % length
    angles = product.astype(jnp.float32) * (2.0 * math.pi / length)
    factor = 1.0 / math.sqrt(length)
    return (jnp.cos(angles) * factor, -jnp.sin(angles) * factor)


def left_apply(table, batch):
    return jnp.einsum("jk,bkl->bjl", table, batch, precision=highest)


def right_apply(batch, table):
    return jnp.einsum("bjk,kl->bjl", batch, table, precision=highest)


def transform(real_in, imag_in, cos_table, sin_table):
    mid_real = left_apply(cos_table, real_in) - left_apply(sin_table, imag_in)
    mid_imag = left_apply(cos_table, imag_in) + left_apply(sin_table, real_in)
    out_real = right_apply(mid_real, cos_table) - right_apply(mid_imag, sin_table)
    out_imag = right_apply(mid_real, sin_table) + right_apply(mid_imag, cos_table)
    return (out_real, out_imag)


def strip_update(
    strip_real,
    strip_imaginary,
    probe,
    measured,
    jitter_rows,
    jitter_cols,
    row_corner,
    column_corner,
):
    patch_len = probe.shape[-1]
    number = measured.shape[0]
    cos_table, sin_table = dft_tables(patch_len)
    starts_row = row_corner + jitter_rows
    starts_col = column_corner + CSTEP * jnp.arange(number, dtype=jnp.int32) + jitter_cols

    def window(image, top, left):
        return lax.dynamic_slice(image, (top, left), (patch_len, patch_len))

    pick = jax.vmap(window, in_axes=(None, 0, 0))
    obj_real = pick(strip_real, starts_row, starts_col)
    obj_imag = pick(strip_imaginary, starts_row, starts_col)
    probe_real = probe[0]
    probe_imag = probe[1]
    wave_real = probe_real * obj_real - probe_imag * obj_imag
    wave_imag = probe_real * obj_imag + probe_imag * obj_real
    far_real, far_imag = transform(wave_real, wave_imag, cos_table, sin_table)
    modulus = jnp.sqrt(far_real * far_real + far_imag * far_imag)
    target = measured.astype(jnp.float32)
    error = modulus - target
    partial_misfit = jnp.sum(error * error)
    ratio = target / jnp.maximum(modulus, floor_value)
    back_real, back_imag = transform(ratio * far_real, ratio * far_imag, cos_table, -sin_table)
    diff_real = back_real - wave_real
    diff_imag = back_imag - wave_imag
    corr_real = probe_real * diff_real + probe_imag * diff_imag
    corr_imag = probe_real * diff_imag - probe_imag * diff_real

    def place(position, sums):
        acc_real, acc_imag = sums
        top = starts_row[position]
        left = starts_col[position]
        acc_real = lax.dynamic_update_slice(
            acc_real, window(acc_real, top, left) + corr_real[position], (top, left)
        )
        acc_imag = lax.dynamic_update_slice(
            acc_imag, window(acc_imag, top, left) + corr_imag[position], (top, left)
        )
        return (acc_real, acc_imag)

    zeros = jnp.zeros(strip_real.shape, strip_real.dtype)
    acc_real, acc_imag = lax.fori_loop(0, number, place, (zeros, zeros))
    return (acc_real, acc_imag, partial_misfit)


def body(volume, path_lengths, probe, measured, jitter, step_sizes):
    group = lax.axis_index("blk")
    groups = lax.axis_size("blk")
    column = lax.axis_index("wide")
    columns = lax.axis_size("wide")
    slab = volume[0]
    row_len = slab.shape[1]
    col_len = slab.shape[2]
    margin = probe.shape[-1] // 2
    own_paths = lax.dynamic_index_in_dim(path_lengths, group, 1, keepdims=False)

    def slab_term(angle, weight):
        coeffs = lax.dynamic_index_in_dim(own_paths, angle, 0, keepdims=False) * weight
        return jnp.einsum("l,lrc->rc", coeffs, slab, precision=highest)

    def cycle_step(section, carried):
        carried = passed_along(carried, "blk", 1)
        angle = (group - section) % groups
        weight = jnp.where(section < groups, 1.0, 0.0).astype(jnp.float32)
        return carried + slab_term(angle, weight)

    projection = lax.fori_loop(
        1, groups + 1, cycle_step, slab_term(group, jnp.ones((), jnp.float32))
    )
    sources = (2, 1, 0, -1, -2)
    pieces_real = []
    pieces_imag = []
    for offset in sources:
        if offset == 0:
            got_phase = projection
        else:
            got_phase = from_behind(projection, "wide", offset)
        source = column - offset
        valid = ((source >= 0) & (source < columns)).astype(jnp.float32)
        pieces_real.append(jnp.cos(got_phase) * valid)
        pieces_imag.append(jnp.sin(got_phase) * valid)
    ext_real = jnp.concatenate(pieces_real, 0)
    ext_imag = jnp.concatenate(pieces_imag, 0)
    strip_real = jnp.pad(ext_real, ((0, 0), (margin, margin)))
    strip_imaginary = jnp.pad(ext_imag, ((0, 0), (margin, margin)))
    row_corner = ROWS_DEV // 4
    column_corner = PATCH // 4 - ROWS_DEV // 4
    acc_real, acc_imag, local_misfit = strip_update(
        strip_real,
        strip_imaginary,
        probe,
        measured[0, 0],
        jitter[0, 0, 0],
        jitter[1, 0, 0],
        row_corner,
        column_corner,
    )
    acc_real = acc_real[:, margin : margin + col_len]
    acc_imag = acc_imag[:, margin : margin + col_len]

    def rows_of(array, slot):
        return array[slot * row_len : (slot + 1) * row_len]

    total_real = rows_of(acc_real, 2)
    total_imag = rows_of(acc_imag, 2)
    for offset in (-2, -1, 1, 2):
        got_real, got_imag = from_behind(
            (rows_of(acc_real, 2 + offset), rows_of(acc_imag, 2 + offset)), "wide", offset
        )
        total_real = total_real + got_real
        total_imag = total_imag + got_imag
    gradient = rows_of(ext_real, 2) * total_imag - rows_of(ext_imag, 2) * total_real
    total_misfit = lax.psum(local_misfit, ("blk", "wide"))
    scaled = step_sizes[:, None] * own_paths
    coeffs = scaled
    update = jnp.einsum(
        "al,arc->lrc",
        coeffs,
        lax.all_gather(gradient[None], "blk", axis=0, tiled=True),
        precision=highest,
    )
    return ((slab - update)[None], total_misfit)


def solution(mesh):
    in_specs = (
        P("blk", None, "wide", None),
        P(),
        P(),
        P("blk", "wide", None, None, None),
        P(None, "blk", "wide", None),
        P(),
    )
    out_specs = (P("blk", None, "wide", None), P())
    return jax.shard_map(body, mesh=mesh, in_specs=in_specs, out_specs=out_specs, check_vma=False)
```

profile of v0, /device:TPU:0, one launch (start us, length us, event | category | flops | bytes accessed | tf_op | source)
XLA Modules:
  0.0 310.6 jit_solution(9081547119739849727)
XLA Ops:
  3.4 11.1 %while.32 = (s32[]{:T(128)}, f32[32,896]{1,0:T(8,128)S(1)}, s32[]{:T(128)}, f32[2,2]{1,0:T(2,128)S(1)}, f32[2,32,896]{2,1,0:T(8,128)S(1)}, /*index=5*/s32[]{:T(128)}, s32[]{:T(128)}, s32[]{:T(128)}, f32[]{:T(128)}, f32[]{:T(128)}) while((s32[]{:T(128)}, f32[32,896]{1,0:T(8,128)S(1)}, s32[]{:T(128)}, f32[2,2]{1,0:T(2,128)S(1)}, ...), condition=%wide.region_1.2_spmd, body=%wide.region_0.1_spmd.sunk | while | flops 716821 | bytes 1147718 | solution.py:126
  3.4 3.0 collective-permute-start
  7.4 2.2 collective-permute-done
  9.6 1.8 collective-permute-start
  12.4 2.1 collective-permute-done
  14.5 3.7 %collective-permute-start.1 = (f32[32,896]{1,0:T(8,128)S(1)}, f32[32,896]{1,0:T(8,128)S(1)}, u32[]{:S(2)}, u32[]{:S(2)}) collective-permute-start(f32[32,896]{1,0:T(8,128)S(1)} %get-tuple-element.260), channel_id=1, source_target_pairs={{0,2},{1,3},{2,4},{3,5},{4,6},{5,7},{6,8},{7,9},{8,10},{9,11},{10,... | collective-permute-start | bytes 344072 | tf_op jit(solution)/shard_map/ppermute | solution.py:23
  24.9 5.7 %collective-permute-done.4 = f32[32,896]{1,0:T(8,128)S(1)} collective-permute-done((f32[32,896]{1,0:T(8,128)S(1)}, f32[32,896]{1,0:T(8,128)S(1)}, u32[]{:S(2)}, u32[]{:S(2)}) %collective-permute-start.4) | collective-permute-done | bytes 114720 | tf_op jit(solution)/shard_map/ppermute | solution.py:23
  31.4 28.7 %while.34 = (s32[]{:T(128)}, f32[160,1024]{1,0:T(8,128)S(1)}, s32[14,2]{0,1:T(2,128)S(1)}, f32[14,128,128]{2,1,0:T(8,128)S(1)}, s32[]{:T(128)}) while((s32[]{:T(128)}, f32[160,1024]{1,0:T(8,128)S(1)}, s32[14,2]{0,1:T(2,128)S(1)}, f32[14,128,128]{2,1,0:T(8,128)S(1)}, s32[]{:T(128)}) %tuple.120), condition=%wide.while_cond, body=%wide.while_body.sunk | while | flops 2 | bytes 131181 | solution.py:67
  60.3 27.1 %while.35 = (s32[]{:T(128)}, f32[160,1024]{1,0:T(8,128)S(1)}, s32[14,2]{0,1:T(2,128)S(1)}, f32[14,128,128]{2,1,0:T(8,128)S(1)}, s32[]{:T(128)}) while((s32[]{:T(128)}, f32[160,1024]{1,0:T(8,128)S(1)}, s32[14,2]{0,1:T(2,128)S(1)}, f32[14,128,128]{2,1,0:T(8,128)S(1)}, s32[]{:T(128)}) %tuple.127), condition=%wide.while_cond.1, body=%wide.while_body.1.sunk | while | flops 2 | bytes 131181 | solution.py:67
  98.2 1.9 convolution_subtract_fusion.2
  100.2 2.6 fusion.13
  102.8 2.2 fusion.14
  105.0 2.2 fusion.18
  107.1 2.2 fusion.8
  111.1 1.9 fusion.38
  113.1 2.2 fusion.7
  117.0 1.9 multiply_subtract_fusion
  119.1 118.2 %while.33 = (s32[]{:T(128)}, f32[160,1024]{1,0:T(8,128)S(1)}, f32[160,1024]{1,0:T(8,128)S(1)}, s32[14]{0:T(128)S(1)}, s32[14]{0:T(128)S(1)}, /*index=5*/f32[14,1...) while((s32[]{:T(128)}, f32[160,1024]{1,0:T(8,128)S(1)}, ...), condition=%wide.region_3.4_spmd, body=%wide.region_2.3_spmd.sunk | while | flops 32776 | bytes 655581 | solution.py:101
  238.8 3.0 collective-permute-start.11
  241.8 4.5 %collective-permute-start.12 = (f32[32,896]{1,0:T(8,128)S(1)}, f32[32,896]{1,0:T(8,128)S(1)}, u32[]{:S(2)}, u32[]{:S(2)}) collective-permute-start(f32[32,896]{1,0:T(8,128)S(1)} %get-tuple-element.348), channel_id=1, source_target_pairs={{0,2},{1,3},{2,4},{3,5},{4,6},{5,7},{6,8},{7,9},{8,10},{9,11},{10,... | collective-permute-start | bytes 344072 | tf_op jit(solution)/shard_map/ppermute | solution.py:23
  249.2 3.5 %collective-permute-start.7 = (f32[32,896]{1,0:T(8,128)S(1)}, f32[32,896]{1,0:T(8,128)S(1)}, u32[]{:S(2)}, u32[]{:S(2)}) collective-permute-start(f32[32,896]{1,0:T(8,128)S(1)} %get-tuple-element.345), channel_id=1, source_target_pairs={{0,1},{1,2},{2,3},{3,4},{4,5},{5,6},{6,7},{7,8},{8,9},{9,10},{10,1... | collective-permute-start | bytes 344072 | tf_op jit(solution)/shard_map/ppermute | solution.py:23
  252.7 4.3 %collective-permute-start.8 = (f32[32,896]{1,0:T(8,128)S(1)}, f32[32,896]{1,0:T(8,128)S(1)}, u32[]{:S(2)}, u32[]{:S(2)}) collective-permute-start(f32[32,896]{1,0:T(8,128)S(1)} %get-tuple-element.344), channel_id=1, source_target_pairs={{0,2},{1,3},{2,4},{3,5},{4,6},{5,7},{6,8},{7,9},{8,10},{9,11},{10,... | collective-permute-start | bytes 344072 | tf_op jit(solution)/shard_map/ppermute | solution.py:23
  258.3 43.2 %psum.7 = f32[]{:T(128)} all-reduce(f32[]{:T(128)} %get-tuple-element.365), channel_id=1, replica_groups=mesh['blk'=2,'wide'=16] {'blk','wide'}, use_global_device_ids=true, to_apply=%region_5.6 | all-reduce | flops 1 | bytes 8 | tf_op jit(solution)/shard_map/psum | solution.py:172
  302.0 5.8 %all-gather = f32[64,896]{1,0:T(8,128)S(1)} all-gather(f32[32,896]{1,0:T(8,128)S(1)} %multiply_subtract_fusion.2), channel_id=2, replica_groups=mesh['blk'=2,'wide'=16] {'blk'}, dimensions={0}, use_global_device_ids=true | all-gather | bytes 344064 | tf_op jit(solution)/shard_map/all_gather | solution.py:178
  (225 shorter events, 156.4 us)
Async XLA Ops:
  0.6 1.2 copy-start
  1.8 0.7 copy-start.1
  3.4 18.8 %copy-start.4 = (f32[2,128,128]{2,1,0:T(8,128)S(1)}, f32[2,128,128]{2,1,0:T(8,128)}, u32[]{:S(2)}) copy-start(f32[2,128,128]{2,1,0:T(8,128)} %param.12) | copy-start | bytes 393220
  3.4 6.2 %collective-permute-start = (f32[32,896]{1,0:T(8,128)S(1)}, f32[32,896]{1,0:T(8,128)S(1)}, u32[]{:S(2)}, u32[]{:S(2)}) collective-permute-start(f32[32,896]{1,0:T(8,128)S(1)} %get-tuple-element.514), channel_id=1, source_target_pairs={{0,16},{16,0},{1,17},{17,1},{2,18},{18,2},{3,19},{19,3},{4,20},{20... | collective-permute-start | bytes 344072 | tf_op jit(solution)/shard_map/while/body/eval_jaxpr/ppermute | solution.py:17
  9.6 4.9 %collective-permute-start = (f32[32,896]{1,0:T(8,128)S(1)}, f32[32,896]{1,0:T(8,128)S(1)}, u32[]{:S(2)}, u32[]{:S(2)}) collective-permute-start(f32[32,896]{1,0:T(8,128)S(1)} %get-tuple-element.514), channel_id=1, source_target_pairs={{0,16},{16,0},{1,17},{17,1},{2,18},{18,2},{3,19},{19,3},{4,20},{20... | collective-permute-start | bytes 344072 | tf_op jit(solution)/shard_map/while/body/eval_jaxpr/ppermute | solution.py:17
  14.5 7.6 %copy-start.5 = (s32[2,1,1,14]{3,2,1,0:T(1,128)S(1)}, s32[2,1,1,14]{3,2,1,0:T(1,128)}, u32[]{:S(2)}) copy-start(s32[2,1,1,14]{3,2,1,0:T(1,128)} %param.14) | copy-start | bytes 340
  14.5 7.7 %collective-permute-start.1 = (f32[32,896]{1,0:T(8,128)S(1)}, f32[32,896]{1,0:T(8,128)S(1)}, u32[]{:S(2)}, u32[]{:S(2)}) collective-permute-start(f32[32,896]{1,0:T(8,128)S(1)} %get-tuple-element.260), channel_id=1, source_target_pairs={{0,2},{1,3},{2,4},{3,5},{4,6},{5,7},{6,8},{7,9},{8,10},{9,11},{10,... | collective-permute-start | bytes 344072 | tf_op jit(solution)/shard_map/ppermute | solution.py:23
  18.2 4.5 %collective-permute-start.2 = (f32[32,896]{1,0:T(8,128)S(1)}, f32[32,896]{1,0:T(8,128)S(1)}, u32[]{:S(2)}, u32[]{:S(2)}) collective-permute-start(f32[32,896]{1,0:T(8,128)S(1)} %get-tuple-element.260), channel_id=1, source_target_pairs={{0,1},{1,2},{2,3},{3,4},{4,5},{5,6},{6,7},{7,8},{8,9},{9,10},{10,1... | collective-permute-start | bytes 344072 | tf_op jit(solution)/shard_map/ppermute | solution.py:23
  19.5 5.0 %collective-permute-start.3 = (f32[32,896]{1,0:T(8,128)S(1)}, f32[32,896]{1,0:T(8,128)S(1)}, u32[]{:S(2)}, u32[]{:S(2)}) collective-permute-start(f32[32,896]{1,0:T(8,128)S(1)} %get-tuple-element.260), channel_id=1, source_target_pairs={{1,0},{2,1},{3,2},{4,3},{5,4},{6,5},{7,6},{8,7},{9,8},{10,9},{11,1... | collective-permute-start | bytes 344072 | tf_op jit(solution)/shard_map/ppermute | solution.py:23
  20.8 9.8 %collective-permute-start.4 = (f32[32,896]{1,0:T(8,128)S(1)}, f32[32,896]{1,0:T(8,128)S(1)}, u32[]{:S(2)}, u32[]{:S(2)}) collective-permute-start(f32[32,896]{1,0:T(8,128)S(1)} %get-tuple-element.260), channel_id=1, source_target_pairs={{2,0},{3,1},{4,2},{5,3},{6,4},{7,5},{8,6},{9,7},{10,8},{11,9},{12,... | collective-permute-start | bytes 344072 | tf_op jit(solution)/shard_map/ppermute | solution.py:23
  98.2 1.9 copy-start.3
  237.5 11.7 %collective-permute-start.10 = (f32[32,896]{1,0:T(8,128)S(1)}, f32[32,896]{1,0:T(8,128)S(1)}, u32[]{:S(2)}, u32[]{:S(2)}) collective-permute-start(f32[32,896]{1,0:T(8,128)S(1)} %get-tuple-element.350), channel_id=1, source_target_pairs={{1,0},{2,1},{3,2},{4,3},{5,4},{6,5},{7,6},{8,7},{9,8},{10,9},{11,1... | collective-permute-start | bytes 344072 | tf_op jit(solution)/shard_map/ppermute | solution.py:23
  238.8 13.9 %collective-permute-start.11 = (f32[32,896]{1,0:T(8,128)S(1)}, f32[32,896]{1,0:T(8,128)S(1)}, u32[]{:S(2)}, u32[]{:S(2)}) collective-permute-start(f32[32,896]{1,0:T(8,128)S(1)} %get-tuple-element.349), channel_id=1, source_target_pairs={{0,1},{1,2},{2,3},{3,4},{4,5},{5,6},{6,7},{7,8},{8,9},{9,10},{10,1... | collective-permute-start | bytes 344072 | tf_op jit(solution)/shard_map/ppermute | solution.py:23
  241.8 15.1 %collective-permute-start.12 = (f32[32,896]{1,0:T(8,128)S(1)}, f32[32,896]{1,0:T(8,128)S(1)}, u32[]{:S(2)}, u32[]{:S(2)}) collective-permute-start(f32[32,896]{1,0:T(8,128)S(1)} %get-tuple-element.348), channel_id=1, source_target_pairs={{0,2},{1,3},{2,4},{3,5},{4,6},{5,7},{6,8},{7,9},{8,10},{9,11},{10,... | collective-permute-start | bytes 344072 | tf_op jit(solution)/shard_map/ppermute | solution.py:23
  246.6 54.9 %collective-permute-start.5 = (f32[32,896]{1,0:T(8,128)S(1)}, f32[32,896]{1,0:T(8,128)S(1)}, u32[]{:S(2)}, u32[]{:S(2)}) collective-permute-start(f32[32,896]{1,0:T(8,128)S(1)} %get-tuple-element.343), channel_id=1, source_target_pairs={{2,0},{3,1},{4,2},{5,3},{6,4},{7,5},{8,6},{9,7},{10,8},{11,9},{12,... | collective-permute-start | bytes 344072 | tf_op jit(solution)/shard_map/ppermute | solution.py:23
  247.9 53.6 %collective-permute-start.6 = (f32[32,896]{1,0:T(8,128)S(1)}, f32[32,896]{1,0:T(8,128)S(1)}, u32[]{:S(2)}, u32[]{:S(2)}) collective-permute-start(f32[32,896]{1,0:T(8,128)S(1)} %get-tuple-element.346), channel_id=1, source_target_pairs={{1,0},{2,1},{3,2},{4,3},{5,4},{6,5},{7,6},{8,7},{9,8},{10,9},{11,1... | collective-permute-start | bytes 344072 | tf_op jit(solution)/shard_map/ppermute | solution.py:23
  249.2 52.3 %collective-permute-start.7 = (f32[32,896]{1,0:T(8,128)S(1)}, f32[32,896]{1,0:T(8,128)S(1)}, u32[]{:S(2)}, u32[]{:S(2)}) collective-permute-start(f32[32,896]{1,0:T(8,128)S(1)} %get-tuple-element.345), channel_id=1, source_target_pairs={{0,1},{1,2},{2,3},{3,4},{4,5},{5,6},{6,7},{7,8},{8,9},{9,10},{10,1... | collective-permute-start | bytes 344072 | tf_op jit(solution)/shard_map/ppermute | solution.py:23
  252.7 48.8 %collective-permute-start.8 = (f32[32,896]{1,0:T(8,128)S(1)}, f32[32,896]{1,0:T(8,128)S(1)}, u32[]{:S(2)}, u32[]{:S(2)}) collective-permute-start(f32[32,896]{1,0:T(8,128)S(1)} %get-tuple-element.344), channel_id=1, source_target_pairs={{0,2},{1,3},{2,4},{3,5},{4,6},{5,7},{6,8},{7,9},{8,10},{9,11},{10,... | collective-permute-start | bytes 344072 | tf_op jit(solution)/shard_map/ppermute | solution.py:23
  257.0 44.5 %collective-permute-start.9 = (f32[32,896]{1,0:T(8,128)S(1)}, f32[32,896]{1,0:T(8,128)S(1)}, u32[]{:S(2)}, u32[]{:S(2)}) collective-permute-start(f32[32,896]{1,0:T(8,128)S(1)} %get-tuple-element.347), channel_id=1, source_target_pairs={{2,0},{3,1},{4,2},{5,3},{6,4},{7,5},{8,6},{9,7},{10,8},{11,9},{12,... | collective-permute-start | bytes 344072 | tf_op jit(solution)/shard_map/ppermute | solution.py:23
  301.9 5.9 %copy-start.2 = (f32[1,2,32,896]{3,1,2,0:T(2,128)S(1)}, f32[1,2,32,896]{3,1,2,0:T(2,128)}, u32[]{:S(2)}) copy-start(f32[1,2,32,896]{3,1,2,0:T(2,128)} %copy-done.1) | copy-start | bytes 688132
  307.8 0.7 copy-start.6
where the time goes:
time: 317 us; the launch traced here: 311 us
  local copies, waits for them, and re-layouts  124 us (39%)
  loops' own time  52.8 us (17%)
  blocking collectives  49 us (15%)
  matrix products  35.1 us (11%)
  starting transfers between devices  32.9 us (10%)
  waiting for transfers between devices  11 us (3%)
  other arithmetic  4.47 us (1%)
    gather x84, local copies, waits for them, and re-layouts  54.7 us
    another operation x1, loops' own time, strip_update(): acc_real, acc_imag = lax.fori_loop(0, number, place, (zeros, zeros))  51.7 us
    psum x1, blocking collectives, body(): total_misfit = lax.psum(local_misfit, ('blk', 'wide'))  43.2 us
    ppermute x12, starting transfers between devices, from_behind(): return lax.ppermute(shard, axis, pairs)  28.1 us
    dynamic_update_slice x14, local copies, waits for them, and re-layouts, place(): lax.dynamic_update_slice(acc_imag, window(acc_imag, top, left) + corr_ima...  23.8 us
    dynamic_update_slice x14, local copies, waits for them, and re-layouts, place(): lax.dynamic_update_slice(acc_real, window(acc_real, top, left) + corr_rea...  23.8 us
    dot_general x8, matrix products, left_apply(): return jnp.einsum('jk,bkl->bjl', table, batch, precision=highest)  15.7 us
    dot_general x8, matrix products, right_apply(): return jnp.einsum('bjk,kl->bjl', batch, table, precision=highest)  15.4 us
  transfers between devices with their start and end apart: 14, of which 4 were waited for; matrix products, arithmetic and copies ran while one was open for 1% of the time, Pallas kernels for 0%

commit v1 on v0

--- a/solution.py
+++ b/solution.py
@@ -169,7 +169,8 @@
         total_real = total_real + got_real
         total_imag = total_imag + got_imag
     gradient = rows_of(ext_real, 2) * total_imag - rows_of(ext_imag, 2) * total_real
-    total_misfit = lax.psum(local_misfit, ("blk", "wide"))
+    parts = lax.all_gather(local_misfit, ("blk", "wide"), axis=0, tiled=False)
+    total_misfit = parts.sum(axis=0)
     scaled = step_sizes[:, None] * own_paths
     coeffs = scaled
     update = jnp.einsum(

time: 317 us -> 329 us (1.038)
  loops' own time: 52.8 us -> 59.8 us
  local copies, waits for them, and re-layouts: 124 us -> 129 us
    psum x1 -> x0, blocking collectives: 43.2 us -> none  [body(): total_misfit = lax.psum(local_misfit, ('blk', 'wide'))]
    unnamed x0 -> x1, blocking collectives: none -> 42.9 us
    another operation x1, loops' own time: 51.7 us -> 58.7 us  [strip_update(): acc_real, acc_imag = lax.fori_loop(0, number, place, (zeros, zeros))]
  transfers between devices with their start and end apart: 14 -> 14, of which waited for: 4 -> 4; matrix products, arithmetic and copies ran while one was open for 1% -> 2% of each run, Pallas kernels for 0% -> 0%
where the time goes in v1:
time: 329 us; the launch traced here: 323 us
  local copies, waits for them, and re-layouts  129 us (39%)
  loops' own time  59.8 us (18%)
  blocking collectives  48.7 us (15%)
  matrix products  35.1 us (11%)
  starting transfers between devices  32.9 us (10%)
  waiting for transfers between devices  11 us (3%)
  other arithmetic  5.07 us (2%)
    another operation x1, loops' own time, strip_update(): acc_real, acc_imag = lax.fori_loop(0, number, place, (zeros, zeros))  58.7 us
    gather x84, local copies, waits for them, and re-layouts  57.7 us
    unnamed x1, blocking collectives  42.9 us
    ppermute x12, starting transfers between devices, from_behind(): return lax.ppermute(shard, axis, pairs)  28 us
    dynamic_update_slice x14, local copies, waits for them, and re-layouts, place(): lax.dynamic_update_slice(acc_imag, window(acc_imag, top, left) + corr_ima...  23.8 us
    dynamic_update_slice x14, local copies, waits for them, and re-layouts, place(): lax.dynamic_update_slice(acc_real, window(acc_real, top, left) + corr_rea...  23.8 us
    dot_general x8, matrix products, left_apply(): return jnp.einsum('jk,bkl->bjl', table, batch, precision=highest)  15.7 us
    dot_general x8, matrix products, right_apply(): return jnp.einsum('bjk,kl->bjl', batch, table, precision=highest)  15.3 us
  transfers between devices with their start and end apart: 14, of which 4 were waited for; matrix products, arithmetic and copies ran while one was open for 2% of the time, Pallas kernels for 0%

profile of v1, /device:TPU:0, one launch (start us, length us, event | category | flops | bytes accessed | tf_op | source)
XLA Modules:
  0.0 323.0 jit_solution(7780633905037322923)
XLA Ops:
  3.4 11.1 %while.32 = (s32[]{:T(128)}, f32[32,896]{1,0:T(8,128)S(1)}, s32[]{:T(128)}, f32[2,2]{1,0:T(2,128)S(1)}, f32[2,32,896]{2,1,0:T(8,128)S(1)}, /*index=5*/s32[]{:T(128)}, s32[]{:T(128)}, s32[]{:T(128)}, f32[]{:T(128)}, f32[]{:T(128)}) while((s32[]{:T(128)}, f32[32,896]{1,0:T(8,128)S(1)}, s32[]{:T(128)}, f32[2,2]{1,0:T(2,128)S(1)}, ...), condition=%wide.region_1.2_spmd, body=%wide.region_0.1_spmd.sunk | while | flops 716821 | bytes 1147718 | solution.py:126
  3.4 3.0 collective-permute-start
  7.4 2.2 collective-permute-done
  9.6 1.8 collective-permute-start
  12.4 2.1 collective-permute-done
  14.5 3.7 %collective-permute-start.1 = (f32[32,896]{1,0:T(8,128)S(1)}, f32[32,896]{1,0:T(8,128)S(1)}, u32[]{:S(2)}, u32[]{:S(2)}) collective-permute-start(f32[32,896]{1,0:T(8,128)S(1)} %get-tuple-element.260), channel_id=1, source_target_pairs={{0,2},{1,3},{2,4},{3,5},{4,6},{5,7},{6,8},{7,9},{8,10},{9,11},{10,... | collective-permute-start | bytes 344072 | tf_op jit(solution)/shard_map/ppermute | solution.py:23
  24.9 5.7 %collective-permute-done.4 = f32[32,896]{1,0:T(8,128)S(1)} collective-permute-done((f32[32,896]{1,0:T(8,128)S(1)}, f32[32,896]{1,0:T(8,128)S(1)}, u32[]{:S(2)}, u32[]{:S(2)}) %collective-permute-start.4) | collective-permute-done | bytes 114720 | tf_op jit(solution)/shard_map/ppermute | solution.py:23
  31.4 29.6 %while.34 = (s32[]{:T(128)}, f32[160,1024]{1,0:T(8,128)S(1)}, s32[14,2]{0,1:T(2,128)S(1)}, f32[14,128,128]{2,1,0:T(8,128)S(1)}, s32[]{:T(128)}) while((s32[]{:T(128)}, f32[160,1024]{1,0:T(8,128)S(1)}, s32[14,2]{0,1:T(2,128)S(1)}, f32[14,128,128]{2,1,0:T(8,128)S(1)}, s32[]{:T(128)}) %tuple.120), condition=%wide.while_cond, body=%wide.while_body.sunk | while | flops 2 | bytes 131181 | solution.py:67
  61.3 29.1 %while.35 = (s32[]{:T(128)}, f32[160,1024]{1,0:T(8,128)S(1)}, s32[14,2]{0,1:T(2,128)S(1)}, f32[14,128,128]{2,1,0:T(8,128)S(1)}, s32[]{:T(128)}) while((s32[]{:T(128)}, f32[160,1024]{1,0:T(8,128)S(1)}, s32[14,2]{0,1:T(2,128)S(1)}, f32[14,128,128]{2,1,0:T(8,128)S(1)}, s32[]{:T(128)}) %tuple.127), condition=%wide.while_cond.1, body=%wide.while_body.1.sunk | while | flops 2 | bytes 131181 | solution.py:67
  101.2 1.9 convolution_subtract_fusion.2
  103.2 2.6 fusion.13
  105.7 2.2 fusion.14
  107.9 2.2 fusion.18
  110.1 2.2 fusion.8
  114.1 1.9 fusion.38
  116.0 2.2 fusion.7
  120.0 1.9 multiply_subtract_fusion
  122.0 126.6 %while.33 = (s32[]{:T(128)}, f32[160,1024]{1,0:T(8,128)S(1)}, f32[160,1024]{1,0:T(8,128)S(1)}, s32[14]{0:T(128)S(1)}, s32[14]{0:T(128)S(1)}, /*index=5*/f32[14,1...) while((s32[]{:T(128)}, f32[160,1024]{1,0:T(8,128)S(1)}, ...), condition=%wide.region_3.4_spmd, body=%wide.region_2.3_spmd.sunk | while | flops 32776 | bytes 655581 | solution.py:101
  250.2 3.0 collective-permute-start.11
  253.2 4.5 %collective-permute-start.12 = (f32[32,896]{1,0:T(8,128)S(1)}, f32[32,896]{1,0:T(8,128)S(1)}, u32[]{:S(2)}, u32[]{:S(2)}) collective-permute-start(f32[32,896]{1,0:T(8,128)S(1)} %get-tuple-element.348), channel_id=1, source_target_pairs={{0,2},{1,3},{2,4},{3,5},{4,6},{5,7},{6,8},{7,9},{8,10},{9,11},{10,... | collective-permute-start | bytes 344072 | tf_op jit(solution)/shard_map/ppermute | solution.py:23
  260.6 3.5 %collective-permute-start.7 = (f32[32,896]{1,0:T(8,128)S(1)}, f32[32,896]{1,0:T(8,128)S(1)}, u32[]{:S(2)}, u32[]{:S(2)}) collective-permute-start(f32[32,896]{1,0:T(8,128)S(1)} %get-tuple-element.345), channel_id=1, source_target_pairs={{0,1},{1,2},{2,3},{3,4},{4,5},{5,6},{6,7},{7,8},{8,9},{9,10},{10,1... | collective-permute-start | bytes 344072 | tf_op jit(solution)/shard_map/ppermute | solution.py:23
  264.0 4.3 %collective-permute-start.8 = (f32[32,896]{1,0:T(8,128)S(1)}, f32[32,896]{1,0:T(8,128)S(1)}, u32[]{:S(2)}, u32[]{:S(2)}) collective-permute-start(f32[32,896]{1,0:T(8,128)S(1)} %get-tuple-element.344), channel_id=1, source_target_pairs={{0,2},{1,3},{2,4},{3,5},{4,6},{5,7},{6,8},{7,9},{8,10},{9,11},{10,... | collective-permute-start | bytes 344072 | tf_op jit(solution)/shard_map/ppermute | solution.py:23
  270.4 42.9 %all-reduce.2 = f32[32]{0:T(128)S(1)} all-reduce(f32[32]{0:T(128)S(1)} %dynamic-update-slice.4), channel_id=1, replica_groups=mesh['blk'=2,'wide'=16] {'blk','wide'}, use_global_device_ids=true, to_apply=%add.2 | all-reduce | flops 32 | bytes 256
  314.4 5.8 %all-gather = f32[64,896]{1,0:T(8,128)S(1)} all-gather(f32[32,896]{1,0:T(8,128)S(1)} %multiply_subtract_fusion.2), channel_id=2, replica_groups=mesh['blk'=2,'wide'=16] {'blk'}, dimensions={0}, use_global_device_ids=true | all-gather | bytes 344064 | tf_op jit(solution)/shard_map/all_gather | solution.py:179
  (228 shorter events, 162.1 us)
Async XLA Ops:
  0.6 1.2 copy-start
  1.8 0.7 copy-start.1
  3.4 18.8 %copy-start.4 = (f32[2,128,128]{2,1,0:T(8,128)S(1)}, f32[2,128,128]{2,1,0:T(8,128)}, u32[]{:S(2)}) copy-start(f32[2,128,128]{2,1,0:T(8,128)} %param.12) | copy-start | bytes 393220
  3.4 6.2 %collective-permute-start = (f32[32,896]{1,0:T(8,128)S(1)}, f32[32,896]{1,0:T(8,128)S(1)}, u32[]{:S(2)}, u32[]{:S(2)}) collective-permute-start(f32[32,896]{1,0:T(8,128)S(1)} %get-tuple-element.514), channel_id=1, source_target_pairs={{0,16},{16,0},{1,17},{17,1},{2,18},{18,2},{3,19},{19,3},{4,20},{20... | collective-permute-start | bytes 344072 | tf_op jit(solution)/shard_map/while/body/eval_jaxpr/ppermute | solution.py:17
  9.6 4.9 %collective-permute-start = (f32[32,896]{1,0:T(8,128)S(1)}, f32[32,896]{1,0:T(8,128)S(1)}, u32[]{:S(2)}, u32[]{:S(2)}) collective-permute-start(f32[32,896]{1,0:T(8,128)S(1)} %get-tuple-element.514), channel_id=1, source_target_pairs={{0,16},{16,0},{1,17},{17,1},{2,18},{18,2},{3,19},{19,3},{4,20},{20... | collective-permute-start | bytes 344072 | tf_op jit(solution)/shard_map/while/body/eval_jaxpr/ppermute | solution.py:17
  14.5 7.6 %copy-start.5 = (s32[2,1,1,14]{3,2,1,0:T(1,128)S(1)}, s32[2,1,1,14]{3,2,1,0:T(1,128)}, u32[]{:S(2)}) copy-start(s32[2,1,1,14]{3,2,1,0:T(1,128)} %param.14) | copy-start | bytes 340
  14.5 7.7 %collective-permute-start.1 = (f32[32,896]{1,0:T(8,128)S(1)}, f32[32,896]{1,0:T(8,128)S(1)}, u32[]{:S(2)}, u32[]{:S(2)}) collective-permute-start(f32[32,896]{1,0:T(8,128)S(1)} %get-tuple-element.260), channel_id=1, source_target_pairs={{0,2},{1,3},{2,4},{3,5},{4,6},{5,7},{6,8},{7,9},{8,10},{9,11},{10,... | collective-permute-start | bytes 344072 | tf_op jit(solution)/shard_map/ppermute | solution.py:23
  18.2 4.5 %collective-permute-start.2 = (f32[32,896]{1,0:T(8,128)S(1)}, f32[32,896]{1,0:T(8,128)S(1)}, u32[]{:S(2)}, u32[]{:S(2)}) collective-permute-start(f32[32,896]{1,0:T(8,128)S(1)} %get-tuple-element.260), channel_id=1, source_target_pairs={{0,1},{1,2},{2,3},{3,4},{4,5},{5,6},{6,7},{7,8},{8,9},{9,10},{10,1... | collective-permute-start | bytes 344072 | tf_op jit(solution)/shard_map/ppermute | solution.py:23
  19.5 5.0 %collective-permute-start.3 = (f32[32,896]{1,0:T(8,128)S(1)}, f32[32,896]{1,0:T(8,128)S(1)}, u32[]{:S(2)}, u32[]{:S(2)}) collective-permute-start(f32[32,896]{1,0:T(8,128)S(1)} %get-tuple-element.260), channel_id=1, source_target_pairs={{1,0},{2,1},{3,2},{4,3},{5,4},{6,5},{7,6},{8,7},{9,8},{10,9},{11,1... | collective-permute-start | bytes 344072 | tf_op jit(solution)/shard_map/ppermute | solution.py:23
  20.8 9.8 %collective-permute-start.4 = (f32[32,896]{1,0:T(8,128)S(1)}, f32[32,896]{1,0:T(8,128)S(1)}, u32[]{:S(2)}, u32[]{:S(2)}) collective-permute-start(f32[32,896]{1,0:T(8,128)S(1)} %get-tuple-element.260), channel_id=1, source_target_pairs={{2,0},{3,1},{4,2},{5,3},{6,4},{7,5},{8,6},{9,7},{10,8},{11,9},{12,... | collective-permute-start | bytes 344072 | tf_op jit(solution)/shard_map/ppermute | solution.py:23
  101.2 1.9 copy-start.3
  248.9 11.7 %collective-permute-start.10 = (f32[32,896]{1,0:T(8,128)S(1)}, f32[32,896]{1,0:T(8,128)S(1)}, u32[]{:S(2)}, u32[]{:S(2)}) collective-permute-start(f32[32,896]{1,0:T(8,128)S(1)} %get-tuple-element.350), channel_id=1, source_target_pairs={{1,0},{2,1},{3,2},{4,3},{5,4},{6,5},{7,6},{8,7},{9,8},{10,9},{11,1... | collective-permute-start | bytes 344072 | tf_op jit(solution)/shard_map/ppermute | solution.py:23
  250.2 13.9 %collective-permute-start.11 = (f32[32,896]{1,0:T(8,128)S(1)}, f32[32,896]{1,0:T(8,128)S(1)}, u32[]{:S(2)}, u32[]{:S(2)}) collective-permute-start(f32[32,896]{1,0:T(8,128)S(1)} %get-tuple-element.349), channel_id=1, source_target_pairs={{0,1},{1,2},{2,3},{3,4},{4,5},{5,6},{6,7},{7,8},{8,9},{9,10},{10,1... | collective-permute-start | bytes 344072 | tf_op jit(solution)/shard_map/ppermute | solution.py:23
  253.2 15.1 %collective-permute-start.12 = (f32[32,896]{1,0:T(8,128)S(1)}, f32[32,896]{1,0:T(8,128)S(1)}, u32[]{:S(2)}, u32[]{:S(2)}) collective-permute-start(f32[32,896]{1,0:T(8,128)S(1)} %get-tuple-element.348), channel_id=1, source_target_pairs={{0,2},{1,3},{2,4},{3,5},{4,6},{5,7},{6,8},{7,9},{8,10},{9,11},{10,... | collective-permute-start | bytes 344072 | tf_op jit(solution)/shard_map/ppermute | solution.py:23
  257.9 55.9 %collective-permute-start.5 = (f32[32,896]{1,0:T(8,128)S(1)}, f32[32,896]{1,0:T(8,128)S(1)}, u32[]{:S(2)}, u32[]{:S(2)}) collective-permute-start(f32[32,896]{1,0:T(8,128)S(1)} %get-tuple-element.343), channel_id=1, source_target_pairs={{2,0},{3,1},{4,2},{5,3},{6,4},{7,5},{8,6},{9,7},{10,8},{11,9},{12,... | collective-permute-start | bytes 344072 | tf_op jit(solution)/shard_map/ppermute | solution.py:23
  259.2 54.6 %collective-permute-start.6 = (f32[32,896]{1,0:T(8,128)S(1)}, f32[32,896]{1,0:T(8,128)S(1)}, u32[]{:S(2)}, u32[]{:S(2)}) collective-permute-start(f32[32,896]{1,0:T(8,128)S(1)} %get-tuple-element.346), channel_id=1, source_target_pairs={{1,0},{2,1},{3,2},{4,3},{5,4},{6,5},{7,6},{8,7},{9,8},{10,9},{11,1... | collective-permute-start | bytes 344072 | tf_op jit(solution)/shard_map/ppermute | solution.py:23
  260.6 53.3 %collective-permute-start.7 = (f32[32,896]{1,0:T(8,128)S(1)}, f32[32,896]{1,0:T(8,128)S(1)}, u32[]{:S(2)}, u32[]{:S(2)}) collective-permute-start(f32[32,896]{1,0:T(8,128)S(1)} %get-tuple-element.345), channel_id=1, source_target_pairs={{0,1},{1,2},{2,3},{3,4},{4,5},{5,6},{6,7},{7,8},{8,9},{9,10},{10,1... | collective-permute-start | bytes 344072 | tf_op jit(solution)/shard_map/ppermute | solution.py:23
  264.0 49.8 %collective-permute-start.8 = (f32[32,896]{1,0:T(8,128)S(1)}, f32[32,896]{1,0:T(8,128)S(1)}, u32[]{:S(2)}, u32[]{:S(2)}) collective-permute-start(f32[32,896]{1,0:T(8,128)S(1)} %get-tuple-element.344), channel_id=1, source_target_pairs={{0,2},{1,3},{2,4},{3,5},{4,6},{5,7},{6,8},{7,9},{8,10},{9,11},{10,... | collective-permute-start | bytes 344072 | tf_op jit(solution)/shard_map/ppermute | solution.py:23
  268.3 45.5 %collective-permute-start.9 = (f32[32,896]{1,0:T(8,128)S(1)}, f32[32,896]{1,0:T(8,128)S(1)}, u32[]{:S(2)}, u32[]{:S(2)}) collective-permute-start(f32[32,896]{1,0:T(8,128)S(1)} %get-tuple-element.347), channel_id=1, source_target_pairs={{2,0},{3,1},{4,2},{5,3},{6,4},{7,5},{8,6},{9,7},{10,8},{11,9},{12,... | collective-permute-start | bytes 344072 | tf_op jit(solution)/shard_map/ppermute | solution.py:23
  314.3 5.9 %copy-start.2 = (f32[1,2,32,896]{3,1,2,0:T(2,128)S(1)}, f32[1,2,32,896]{3,1,2,0:T(2,128)}, u32[]{:S(2)}) copy-start(f32[1,2,32,896]{3,1,2,0:T(2,128)} %copy-done.1) | copy-start | bytes 688132
  320.2 0.7 copy-start.6
